TPU v7x, 32 devices: a whole 2x2x4 slice. The times are simulated.
32 devices in a mesh: batch: 4 (over y, x), mp: 8 (over z, core).
Axes of the slice: x: 2, y: 2, z: 4, core: 2. Of those that a mesh axis runs over, the one named last changes fastest.
Arguments:
- queries: bfloat16 [8192, 768], P(('batch', 'mp')), may hold values from -2 to 2
- docs: bfloat16 [8192, 768], P(('batch', 'mp')), may hold values from -2 to 2
- doc_id: int32 [8192], P(('batch', 'mp')), may hold values from 0 to 4095, as said below
- owner_row: int32 [4096], P(('batch', 'mp')), may hold values from 0 to 4095, as said below
Outputs:
- query_grad: bfloat16 [8192, 768], P(('batch', 'mp'))
- doc_grad: bfloat16 [4096, 768], P(('batch', 'mp'))
- loss: float32 [], replicated
Inputs may be any that keep to these rules, and one draw needn't show every extreme that they name: `doc_id`: pairs may share a document; document u is held by block u // 128 of the table; the pairs of a device name documents of blocks of its own batch index only; no more than 64 pairs of one device name documents of one block, and on every device some block is named by exactly 64 of its pairs. `owner_row`: distinct rows; the row of document u lies in rows (u // 128) * 128 to (u // 128) * 128 + 127.
All inputs are finite; a program needn't handle non-finite values.
Results may differ from a plain program's by a relative error of at most 0.003.
Values may be sent and summed in bfloat16 or wider, within the bound.
A program may use at most 64 MiB of HBM per device.

v0:
```python
import functools

import jax
import jax.numpy as jnp
from jax import lax
from jax.experimental import pallas as pl
from jax.experimental.pallas import tpu as pltpu
from jax.sharding import PartitionSpec as P

inverse_temp = 80.0
f32 = jnp.float32
bf16 = jnp.bfloat16
NT = (((1,), (1,)), ((), ()))
NN = (((1,), (0,)), ((), ()))
TN = (((0,), (0,)), ((), ()))


def dot(x, y, dims=NN):
    return lax.dot_general(x, y, dims, preferred_element_type=f32)


def iota(shape, dim):
    return lax.broadcasted_iota(jnp.int32, shape, dim)


def send(src, dst, send_sem, recv_sem, device):
    pltpu.make_async_remote_copy(
        src_ref=src,
        dst_ref=dst,
        send_sem=send_sem,
        recv_sem=recv_sem,
        device_id=device,
        device_id_type=pl.DeviceIdType.MESH,
    ).start()


def partner(m, k, n):
    if n & (n - 1):
        return (m + k) % n
    bit = 1
    while bit < n:
        if k & bit:
            m = m + bit * (1 - 2 * ((m // bit) % 2))
        bit *= 2
    return m


def wait(ref, sem):
    pltpu.make_async_copy(ref, ref, sem).wait()


def kernel(
    n_a, n_b, n_mp, slots, n_ch,
    q_hbm, d_hbm, id_hbm, own_hbm,
    qg_ref, dg_ref, loss_ref,
    qbuf, dbuf, st, gt, stat_own, stat_buf,
    qg_send, qg_buf, pg_send, pg_buf, zsend, zbuf,
    ids_buf, place_t, place, pick, loss_b, loss_m, loss_own, loss_grp,
    q_ref, d_ref, id_ref, own_ref,
    q_ss, q_rs, d_ss, d_rs, s_ss, s_rs, qg_ss, qg_rs, pg_ss, pg_rs,
    z_ss, z_rs, id_ss, id_rs, l_ss, l_rs, in_sem,
):
    rows, width = q_ref.shape
    own_rows = own_ref.shape[1]
    cw = width // n_ch
    n_batch = n_a * n_b
    me_b = lax.axis_index("batch")
    me_m = lax.axis_index("mp")
    a = me_b // n_b
    c = me_b % n_b

    def row_peer(j):
        return {"batch": a * n_b + (c + j) % n_b, "mp": me_m}

    def col_peer(i):
        return {"batch": ((a + i) % n_a) * n_b + c, "mp": me_m}

    def batch_peer(t):
        return {"batch": (me_b + t) % n_batch, "mp": me_m}

    def mp_peer(k):
        return {"batch": me_b, "mp": partner(me_m, k, n_mp)}

    load_q = pltpu.make_async_copy(q_hbm, q_ref, in_sem.at[0])
    load_d = pltpu.make_async_copy(d_hbm, d_ref, in_sem.at[1])
    load_id = pltpu.make_async_copy(id_hbm, id_ref, in_sem.at[2])
    load_own = pltpu.make_async_copy(own_hbm, own_ref, in_sem.at[3])
    loads = (load_q, load_d, load_id, load_own)
    for load in loads:
        load.start()

    barrier = pltpu.get_barrier_semaphore()
    for t in range(1, n_batch):
        pl.semaphore_signal(
            barrier, inc=1, device_id=batch_peer(t), device_id_type=pl.DeviceIdType.MESH
        )
    for k in range(1, n_mp):
        pl.semaphore_signal(
            barrier, inc=1, device_id=mp_peer(k), device_id_type=pl.DeviceIdType.MESH
        )
    pl.semaphore_wait(barrier, n_batch + n_mp - 2)
    for load in loads:
        load.wait()

    for j in range(1, n_b):
        to = n_b - j - 1
        send(q_ref, qbuf.at[to], q_ss.at[j - 1], q_rs.at[to], row_peer(j))
    for i in range(1, n_a):
        to = n_a - i - 1
        send(d_ref, dbuf.at[to], d_ss.at[i - 1], d_rs.at[to], col_peer(i))
    for k in range(1, n_mp):
        send(id_ref, ids_buf.at[k - 1], id_ss, id_rs, mp_peer(k))

    eye = iota((rows, rows), 0) == iota((rows, rows), 1)
    s00 = dot(d_ref[...], q_ref[...], NT) * inverse_temp
    st[0, 0] = s00
    own_score = jnp.sum(jnp.where(eye, s00, 0.0), axis=0, keepdims=True)

    upper = (iota((rows, rows), 0) < iota((rows, rows), 1)).astype(bf16)
    which = iota((n_mp, rows), 0)
    if n_mp & (n_mp - 1):
        col = me_m + which
        col = jnp.where(col >= n_mp, col - n_mp, col)
    else:
        col = jnp.broadcast_to(me_m, which.shape) ^ which
    first = (me_b * n_mp + col) * own_rows
    ids = jnp.broadcast_to(id_ref[...], (n_mp, rows))
    mask = ((ids >= first) & (ids < first + own_rows)).astype(f32)
    rank = dot(mask.astype(bf16), upper)
    count = jnp.sum(mask, axis=1, keepdims=True)
    first_slot = (which * slots).astype(f32)
    slot = jnp.sum(mask * (rank + first_slot), axis=0, keepdims=True)
    free = mask * (rank + count < slots).astype(f32)
    spare = jnp.sum(free * (rank + count + first_slot + 1.0), axis=0, keepdims=True) - 1.0
    at = iota((n_mp * slots, rows), 0)
    pick[:, pl.ds(0, rows)] = (at == slot.astype(jnp.int32)).astype(f32).astype(bf16)
    pick[:, pl.ds(rows, rows)] = (at == spare.astype(jnp.int32)).astype(f32).astype(bf16)

    base = (me_b * n_mp + me_m) * own_rows
    owner = (iota((own_rows, own_rows), 0) == own_ref[...] - base).astype(f32).astype(bf16)

    def place_block(k, ids_k):
        local = ids_k - base
        here = ((local >= 0) & (local < own_rows)).astype(f32)
        doc = (iota((own_rows, rows), 0) == local).astype(f32).astype(bf16)
        target = dot(owner, doc).astype(bf16)
        rank_k = dot(jnp.broadcast_to(here, (8, rows)).astype(bf16), upper)[0:1]
        spare_k = rank_k + jnp.sum(here, axis=1, keepdims=True)
        rank_k = jnp.where(here > 0.0, rank_k, -1.0).astype(jnp.int32)
        spare_k = jnp.where(here > 0.0, spare_k, -1.0).astype(jnp.int32)
        at_k = iota((slots, rows), 0)
        taken = ((at_k == rank_k) | (at_k == spare_k)).astype(f32).astype(bf16)
        place_t[pl.ds(k * slots, slots), :] = dot(taken, target, NT)

    place_block(0, id_ref[...])
    wait(ids_buf, id_rs)
    for k in range(1, n_mp):
        place_block(k, ids_buf[k - 1])
    place[...] = jnp.transpose(place_t[...]).astype(bf16)

    def q_of(j):
        return q_ref if j == 0 else qbuf.at[j - 1]

    def d_of(i):
        return d_ref if i == 0 else dbuf.at[i - 1]

    for i in range(1, n_a):
        wait(dbuf.at[i - 1], d_rs.at[i - 1])
        st[i, 0] = dot(d_of(i)[...], q_ref[...], NT) * inverse_temp
    for j in range(1, n_b):
        wait(qbuf.at[j - 1], q_rs.at[j - 1])
        for i in range(n_a):
            st[i, j] = dot(d_of(i)[...], q_of(j)[...], NT) * inverse_temp

    for j in range(n_b):
        top = jnp.max(st[0, j], axis=0, keepdims=True)
        for i in range(1, n_a):
            top = jnp.maximum(top, jnp.max(st[i, j], axis=0, keepdims=True))
        total = jnp.zeros_like(top)
        for i in range(n_a):
            e = jnp.exp(st[i, j] - top)
            st[i, j] = e
            total = total + jnp.sum(e, axis=0, keepdims=True)
        stat_own[pl.ds(2 * j, 1), :] = top
        stat_own[pl.ds(2 * j + 1, 1), :] = total
    for j in range(1, n_b):
        to = n_b - j - 1
        send(stat_own, stat_buf.at[to], s_ss.at[j - 1], s_rs.at[to], row_peer(j))
    for j in range(1, n_b):
        wait(stat_buf.at[j - 1], s_rs.at[j - 1])

    for j in range(n_b):
        tops = [stat_own[pl.ds(2 * j, 1), :]]
        totals = [stat_own[pl.ds(2 * j + 1, 1), :]]
        for s in range(1, n_b):
            r = (j - s) % n_b
            tops.append(stat_buf[s - 1, pl.ds(2 * r, 1), :])
            totals.append(stat_buf[s - 1, pl.ds(2 * r + 1, 1), :])
        top = functools.reduce(jnp.maximum, tops)
        total = sum(t * jnp.exp(m - top) for m, t in zip(tops, totals))
        scale = jnp.exp(tops[0] - top) / total
        if j == 0:
            part = jnp.sum(top + jnp.log(total) - own_score, axis=1, keepdims=True)
            loss_own[...] = jnp.broadcast_to(part, loss_own.shape)
            loss_b[me_b] = loss_own[...]
            for t in range(1, n_batch):
                send(loss_own, loss_b.at[me_b], l_ss.at[0], l_rs.at[0], batch_peer(t))
        for i in range(n_a):
            p = st[i, j] * scale
            if i == 0 and j == 0:
                p = p - eye.astype(f32)
            gt[i, j] = p.astype(bf16)

    def pair_part(i, ch):
        at = pl.ds(ch * cw, cw)
        return sum(dot(gt[i, j], q_of(j)[:, at]) for j in range(n_b)) * inverse_temp

    def query_part(j):
        return sum(dot(gt[i, j], d_of(i)[...], TN) for i in range(n_a)) * inverse_temp

    for ch in range(n_ch):
        for i in range(1, n_a):
            to = n_a - i - 1
            pg_send[i - 1, ch] = pair_part(i, ch).astype(bf16)
            send(
                pg_send.at[i - 1, ch], pg_buf.at[to, ch],
                pg_ss.at[i - 1, ch], pg_rs.at[to, ch], col_peer(i),
            )
    for j in range(1, n_b):
        to = n_b - j - 1
        qg_send[j - 1] = query_part(j).astype(bf16)
        send(qg_send.at[j - 1], qg_buf.at[to], qg_ss.at[j - 1], qg_rs.at[to], row_peer(j))

    wait(loss_b.at[pl.ds(0, n_batch - 1)], l_rs.at[0])
    loss_grp[...] = jnp.sum(loss_b[...], axis=0)
    for k in range(1, n_mp):
        send(loss_grp, loss_m.at[me_m], l_ss.at[1], l_rs.at[1], mp_peer(k))
    loss_m[me_m] = loss_grp[...]

    for ch in range(n_ch):
        part = pair_part(0, ch)
        for i in range(1, n_a):
            wait(pg_buf.at[i - 1, ch], pg_rs.at[i - 1, ch])
            part = part + pg_buf[i - 1, ch].astype(f32)
        high = part.astype(bf16)
        low = (part - high.astype(f32)).astype(bf16)
        zsend[ch] = dot(pick[...], jnp.concatenate([high, low], axis=0)).astype(bf16)
        for k in reversed(range(1, n_mp)):
            at = pl.ds(k * slots, slots)
            send(zsend.at[ch, at], zbuf.at[ch, at], z_ss.at[ch], z_rs.at[ch], mp_peer(k))
        zbuf[ch, pl.ds(0, slots)] = zsend[ch, pl.ds(0, slots)]

    grad = query_part(0)
    for j in range(1, n_b):
        wait(qg_buf.at[j - 1], qg_rs.at[j - 1])
        grad = grad + qg_buf[j - 1].astype(f32)
    qg_ref[...] = grad.astype(bf16)

    wait(loss_m.at[pl.ds(0, n_mp - 1)], l_rs.at[1])
    loss_sum = jnp.sum(loss_m[...], axis=0)
    loss_ref[0, 0] = jnp.max(loss_sum) / (rows * n_batch * n_mp)

    for ch in range(n_ch):
        wait(zbuf.at[ch, pl.ds(slots, (n_mp - 1) * slots)], z_rs.at[ch])
        dg_ref[:, pl.ds(ch * cw, cw)] = dot(place[...], zbuf[ch]).astype(bf16)

    for j in range(1, n_b):
        wait(q_ref, q_ss.at[j - 1])
        wait(stat_own, s_ss.at[j - 1])
        wait(qg_send.at[j - 1], qg_ss.at[j - 1])
    for i in range(1, n_a):
        wait(d_ref, d_ss.at[i - 1])
        for ch in range(n_ch):
            wait(pg_send.at[i - 1, ch], pg_ss.at[i - 1, ch])
    wait(ids_buf, id_ss)
    for ch in range(n_ch):
        wait(zsend.at[ch, pl.ds(slots, (n_mp - 1) * slots)], z_ss.at[ch])
    wait(loss_b.at[pl.ds(0, n_batch - 1)], l_ss.at[0])
    wait(loss_m.at[pl.ds(0, n_mp - 1)], l_ss.at[1])


def place_outputs(qg_ref, dg_ref, qg_out, dg_out, sem):
    copies = [
        pltpu.make_async_copy(qg_ref, qg_out, sem.at[0]),
        pltpu.make_async_copy(dg_ref, dg_out, sem.at[1]),
    ]
    for copy in copies:
        copy.start()
    for copy in copies:
        copy.wait()


def per_device(n_batch, n_mp, queries, docs, doc_id, owner_row):
    rows, width = queries.shape
    own_rows = owner_row.shape[0]
    n_a = next(x for x in range(1, n_batch + 1) if n_batch % x == 0 and x * x >= n_batch)
    n_b = n_batch // n_a
    slots = max(16, -(-2 * rows // n_mp // 16) * 16)
    n_ch = max(1, width // 128)
    cw = width // n_ch
    vmem = pl.BlockSpec(memory_space=pltpu.VMEM)
    dma = pltpu.SemaphoreType.DMA
    ra, rb = max(n_a - 1, 1), max(n_b - 1, 1)
    query_grad, doc_grad, loss = pl.pallas_call(
        functools.partial(kernel, n_a, n_b, n_mp, slots, n_ch),
        out_shape=(
            jax.ShapeDtypeStruct((rows, width), bf16),
            jax.ShapeDtypeStruct((own_rows, width), bf16),
            jax.ShapeDtypeStruct((1, 1), f32),
        ),
        in_specs=[pl.BlockSpec(memory_space=pltpu.HBM)] * 4,
        out_specs=(vmem, vmem, pl.BlockSpec(memory_space=pltpu.SMEM)),
        scratch_shapes=[
            pltpu.VMEM((rb, rows, width), bf16),
            pltpu.VMEM((ra, rows, width), bf16),
            pltpu.VMEM((n_a, n_b, rows, rows), f32),
            pltpu.VMEM((n_a, n_b, rows, rows), bf16),
            pltpu.VMEM((2 * n_b, rows), f32),
            pltpu.VMEM((rb, 2 * n_b, rows), f32),
            pltpu.VMEM((rb, rows, width), bf16),
            pltpu.VMEM((rb, rows, width), bf16),
            pltpu.VMEM((ra, n_ch, rows, cw), bf16),
            pltpu.VMEM((ra, n_ch, rows, cw), bf16),
            pltpu.VMEM((n_ch, n_mp * slots, cw), bf16),
            pltpu.VMEM((n_ch, n_mp * slots, cw), bf16),
            pltpu.VMEM((n_mp - 1, 1, rows), jnp.int32),
            pltpu.VMEM((n_mp * slots, own_rows), f32),
            pltpu.VMEM((own_rows, n_mp * slots), bf16),
            pltpu.VMEM((n_mp * slots, 2 * rows), bf16),
            pltpu.VMEM((n_batch, 1, 128), f32),
            pltpu.VMEM((n_mp, 1, 128), f32),
            pltpu.VMEM((1, 128), f32),
            pltpu.VMEM((1, 128), f32),
            pltpu.VMEM((rows, width), bf16),
            pltpu.VMEM((rows, width), bf16),
            pltpu.VMEM((1, rows), jnp.int32),
            pltpu.VMEM((1, own_rows), jnp.int32),
            dma((rb,)), dma((rb,)), dma((ra,)), dma((ra,)), dma((rb,)), dma((rb,)),
            dma((rb,)), dma((rb,)), dma((ra, n_ch)), dma((ra, n_ch)),
            dma((n_ch,)), dma((n_ch,)), dma, dma, dma((2,)), dma((2,)), dma((4,)),
        ],
        compiler_params=pltpu.CompilerParams(
            collective_id=0, has_side_effects=True, vmem_limit_bytes=32 * 1024 * 1024
        ),
    )(queries, docs, doc_id.reshape(1, rows), owner_row.reshape(1, own_rows))
    hbm = pl.BlockSpec(memory_space=pl.ANY)
    query_grad, doc_grad = pl.pallas_call(
        place_outputs,
        out_shape=(
            jax.ShapeDtypeStruct((rows, width), bf16),
            jax.ShapeDtypeStruct((own_rows, width), bf16),
        ),
        in_specs=[vmem] * 2,
        out_specs=(hbm, hbm),
        scratch_shapes=[dma((2,))],
        compiler_params=pltpu.CompilerParams(vmem_limit_bytes=4 * 1024 * 1024),
    )(query_grad, doc_grad)
    return query_grad, doc_grad, loss.reshape(())


def solution(mesh):
    in_specs = (
        P(("batch", "mp"), None),
        P(("batch", "mp"), None),
        P(("batch", "mp")),
        P(("batch", "mp")),
    )
    out_specs = (P(("batch", "mp"), None), P(("batch", "mp"), None), P())
    body = functools.partial(per_device, mesh.shape["batch"], mesh.shape["mp"])
    return jax.shard_map(
        body, mesh=mesh, in_specs=in_specs, out_specs=out_specs, check_vma=False
    )
```

profile of v0, /device:TPU:0, one launch (start us, length us, event | category | flops | bytes accessed | tf_op | source)
XLA Modules:
  0.0 47.1 jit_solution(14092728926176597601)
XLA Ops:
  0.6 0.0 copy-start.2
  0.6 0.0 copy-start.3
  0.7 0.7 %copy-done.2 = s32[256]{0:T(256)S(1)} copy-done((s32[256]{0:T(256)S(1)}, s32[256]{0:T(256)}, u32[]{:S(2)}) %copy-start.2) | copy-done | bytes 1048
  1.3 0.0 copy-done.3
  1.3 0.0 copy-start
  1.3 1.0 %copy-done = bf16[256,768]{1,0:T(8,128)(2,1)S(1)} copy-done((bf16[256,768]{1,0:T(8,128)(2,1)S(1)}, bf16[256,768]{1,0:T(8,128)(2,1)}, u32[]{:S(2)}) %copy-start) | copy-done | bytes 393240
  2.3 0.0 copy-start.1
  2.3 1.0 %copy-done.1 = bf16[256,768]{1,0:T(8,128)(2,1)S(1)} copy-done((bf16[256,768]{1,0:T(8,128)(2,1)S(1)}, bf16[256,768]{1,0:T(8,128)(2,1)}, u32[]{:S(2)}) %copy-start.1) | copy-done | bytes 393240
  3.3 41.3 %shard_map.67 = (bf16[256,768]{1,0:T(8,128)(2,1)S(1)}, bf16[128,768]{1,0:T(8,128)(2,1)S(1)}, f32[1,1]{1,0:T(1,128)}) custom-call(bf16[256,768]{1,0:T(8,128)(2,1)S(1)} %copy-done, bf16[256,768]{1,0:T(8,128)(2,1)S(1)} %copy-done.1, s32[1,256]{1,0:T(1,128)S(1)} %bitcast.3, s32[1,128]{1,0:T(1,128)S(1)} %bitcast.4), custom_call_target="tpu_custom_call" | custom-call | tf_op jit(solution)/shard_map/pallas_call | solution.py:304
  44.6 0.8 %shard_map.68 = (bf16[256,768]{1,0:T(8,128)(2,1)}, bf16[128,768]{1,0:T(8,128)(2,1)}) custom-call(bf16[256,768]{1,0:T(8,128)(2,1)S(1)} %get-tuple-element.8.qg_ref, bf16[128,768]{1,0:T(8,128)(2,1)S(1)} %get-tuple-element.9.dg_ref), custom_call_target="tpu_custom_call" | custom-call | tf_op jit(solution)/shard_map/pallas_call | solution.py:347
Async XLA Ops:
  0.6 0.7 %copy-start.2 = (s32[256]{0:T(256)S(1)}, s32[256]{0:T(256)}, u32[]{:S(2)}) copy-start(s32[256]{0:T(256)} %param.6) | copy-start | bytes 3076
  0.6 0.7 %copy-start.3 = (s32[128]{0:T(128)S(1)}, s32[128]{0:T(128)}, u32[]{:S(2)}) copy-start(s32[128]{0:T(128)} %param.7) | copy-start | bytes 1540
  1.3 1.0 %copy-start = (bf16[256,768]{1,0:T(8,128)(2,1)S(1)}, bf16[256,768]{1,0:T(8,128)(2,1)}, u32[]{:S(2)}) copy-start(bf16[256,768]{1,0:T(8,128)(2,1)} %q_hbm.1) | copy-start | bytes 1179652
  2.3 1.0 %copy-start.1 = (bf16[256,768]{1,0:T(8,128)(2,1)S(1)}, bf16[256,768]{1,0:T(8,128)(2,1)}, u32[]{:S(2)}) copy-start(bf16[256,768]{1,0:T(8,128)(2,1)} %d_hbm.1) | copy-start | bytes 1179652
where the time goes:
time: 47.3 us; the launch traced here: 47.1 us
  Pallas kernels  42.1 us (89%)
  local copies, waits for them, and re-layouts  2.66 us (6%)
  between operations  2.35 us (5%)
    pallas_call x1, Pallas kernels, per_device(): pl.pallas_call(functools.partial(kernel, n_a, n_b, n_mp, slots, n_ch), ou...  41.3 us
    unnamed x8, local copies, waits for them, and re-layouts  2.66 us

commit v1 on v0

--- a/solution.py
+++ b/solution.py
@@ -342,7 +342,7 @@
         compiler_params=pltpu.CompilerParams(
             collective_id=0, has_side_effects=True, vmem_limit_bytes=32 * 1024 * 1024
         ),
-    )(queries, docs, doc_id.reshape(1, rows), owner_row.reshape(1, own_rows))
+    )(*(pltpu.with_memory_space_constraint(x, pltpu.HBM) for x in (queries, docs, doc_id.reshape(1, rows), owner_row.reshape(1, own_rows))))
     hbm = pl.BlockSpec(memory_space=pl.ANY)
     query_grad, doc_grad = pl.pallas_call(
         place_outputs,

time: 47.3 us -> 44.3 us (0.937)
  local copies, waits for them, and re-layouts: 2.66 us -> 0 us
    unnamed x8 -> x0, local copies, waits for them, and re-layouts: 2.66 us -> none
where the time goes in v1:
time: 44.3 us; the launch traced here: 44.2 us
  Pallas kernels  41.8 us (94%)
  between operations  2.4 us (5%)
    pallas_call x1, Pallas kernels, per_device(): pl.pallas_call(functools.partial(kernel, n_a, n_b, n_mp, slots, n_ch), ou...  40.9 us

profile of v1, /device:TPU:0, one launch (start us, length us, event | category | flops | bytes accessed | tf_op | source)
XLA Modules:
  0.0 44.2 jit_solution(4031114239514519473)
XLA Ops:
  0.6 40.9 %shard_map.67 = (bf16[256,768]{1,0:T(8,128)(2,1)S(1)}, bf16[128,768]{1,0:T(8,128)(2,1)S(1)}, f32[1,1]{1,0:T(1,128)}) custom-call(bf16[256,768]{1,0:T(8,128)(2,1)} %q_hbm.1, bf16[256,768]{1,0:T(8,128)(2,1)} %d_hbm.1, s32[1,256]{1,0:T(1,128)} %bitcast.3, s32[1,128]{1,0:T(1,128)} %bitcast.4), custom_call_target="tpu_custom_call" | custom-call | tf_op jit(solution)/shard_map/pallas_call | solution.py:304
  41.6 0.8 %shard_map.68 = (bf16[256,768]{1,0:T(8,128)(2,1)}, bf16[128,768]{1,0:T(8,128)(2,1)}) custom-call(bf16[256,768]{1,0:T(8,128)(2,1)S(1)} %get-tuple-element.8.qg_ref, bf16[128,768]{1,0:T(8,128)(2,1)S(1)} %get-tuple-element.9.dg_ref), custom_call_target="tpu_custom_call" | custom-call | tf_op jit(solution)/shard_map/pallas_call | solution.py:347
